TPU v7x, 128 devices: a whole 4x4x4 slice. The times are simulated.
128 devices in a mesh: gx: 8 (over y_lo, x), gy: 8 (over z, core), gz: 2 (over y_hi).
Axes of the slice: x: 4, y: 4 (y_hi: 2, y_lo: 2; y = y_hi * 2 + y_lo), z: 4, core: 2. Of those that a mesh axis runs over, the one named last changes fastest.
Arguments:
- blocks: int32 [131072, 4], P(('gx', 'gy', 'gz')), may hold values from 0 to 15, as said below
- coefficients: bfloat16 [131072, 4, 128], P(('gx', 'gy', 'gz')), may hold values from -80 to 80
- residuals: float32 [131072], P(('gx', 'gy', 'gz')), may hold values from -3000 to 3000
Outputs:
- factor: float32 [8, 2, 128, 8, 2, 128], P('gx', None, None, 'gy')
- solution: float32 [16, 128], replicated
Inputs may be any that keep to these rules, and one draw needn't show every extreme that they name: Each row names 4 different blocks.
All inputs are finite; a program needn't handle non-finite values.
Results may differ from a plain program's by a relative error of at most 0.0003.
Values sent between devices are 32-bit elements; how exact they have to be, the bound alone decides.
No kernel may reach another device: no remote copies, remote signals or barrier semaphores. Data moves between devices by JAX's collectives and lax.ppermute only.
A program may use at most 128 MiB of HBM per device.

v0:
```python
import jax
import jax.numpy as jnp
from jax import lax
from jax.sharding import PartitionSpec as P

G = 2048
BS = 128


def picked(x, axis, root):
    return lax.dynamic_index_in_dim(lax.all_gather(x, axis), root, 0, keepdims=False)


def laid_out(pieces, dim):
    shape = list(pieces.shape[1:])
    shape[dim] *= pieces.shape[0]
    return jnp.moveaxis(pieces, 0, dim).reshape(shape)


def copy_for_each(x, axis):
    size = lax.axis_size(axis)
    return lax.all_to_all(jnp.broadcast_to(x[None], (size, *x.shape)), axis, 0, 0, tiled=True)


def gather_directly(x, axis, dim):
    return laid_out(copy_for_each(x, axis), dim)


def on_device(blocks, coefficients, residuals):
    row_count = lax.axis_size("gx")
    col_count = lax.axis_size("gy")
    row_index = lax.axis_index("gx")
    col_index = lax.axis_index("gy")
    scale = 1.0 / (coefficients.shape[0] * row_count * col_count * lax.axis_size("gz"))
    width = coefficients.shape[2]
    nblock = G // BS
    per_dev = nblock // row_count
    target = (
        jnp.arange(per_dev, dtype=jnp.int32)[None, :] * row_count
        + jnp.arange(row_count, dtype=jnp.int32)[:, None]
    ).reshape(-1)
    placed = (blocks[:, :, None] == target[None, None, :]).astype(jnp.bfloat16)
    design = jnp.einsum("osz,osx->ozx", placed, coefficients, preferred_element_type=jnp.float32)
    design = design.astype(jnp.bfloat16).reshape(-1, row_count, per_dev, width)
    natural = (blocks[:, :, None] == jnp.arange(nblock, dtype=jnp.int32)[None, None, :]).astype(
        jnp.float32
    )
    weighted = coefficients.astype(jnp.float32) * residuals[:, None, None]
    rhs_local = (
        jnp.einsum("osb,osx->bx", natural, weighted, precision=lax.Precision.HIGHEST) * scale
    )
    rhs = lax.psum(rhs_local, ("gx", "gy", "gz"))
    row_span = min(row_count, (1 * lax.axis_size(("gx", "gy")) - 1) // col_count + 2)
    blockwise = (
        jnp.einsum("opix,oqjy->pqixjy", design, design, preferred_element_type=jnp.float32) * scale
    )
    blockwise = blockwise.reshape(row_span * col_count, per_dev, width, per_dev, width)
    summed = lax.psum_scatter(blockwise, ("gx", "gy"), scatter_dimension=0, tiled=True)
    summed = lax.psum(summed, "gz")
    matrix = summed.reshape(per_dev, width, per_dev, width)
    zero = jnp.zeros((), jnp.int32)
    block_ids = (
        jnp.arange(per_dev, dtype=jnp.int32)[None, :] * row_count
        + jnp.arange(row_count, dtype=jnp.int32)[:, None]
    )

    def factor_step(step, state):
        working, factor, pivots = state
        step_row = step % row_count
        step_local_row = step // row_count
        step_col = step % col_count
        step_local_col = step // col_count
        column = lax.dynamic_slice(
            working, (zero, zero, step_local_col, zero), (per_dev, width, 1, width)
        ).reshape(per_dev, width, width)
        row_raw = picked(column, "gy", step_col)
        whole = gather_directly(row_raw, "gx", 0).reshape(row_count, per_dev, width, width)
        own_diag = lax.dynamic_slice(
            whole, (step_row, step_local_row, zero, zero), (1, 1, width, width)
        ).reshape(width, width)
        chol = jnp.linalg.cholesky(own_diag)
        stacked = whole.transpose(3, 0, 1, 2).reshape(width, row_count * per_dev * width)
        solved = jax.scipy.linalg.solve_triangular(chol, stacked, lower=True)
        panel_all = solved.reshape(width, row_count, per_dev, width).transpose(1, 2, 3, 0)
        panel_all = jnp.where((block_ids > step)[:, :, None, None], panel_all, 0.0)
        row_panel = lax.dynamic_index_in_dim(panel_all, row_index, 0, keepdims=False)
        col_panel = lax.dynamic_index_in_dim(panel_all, col_index, 0, keepdims=False)
        working = working - jnp.einsum(
            "rxk,cyk->rxcy", row_panel, col_panel, precision=lax.Precision.HIGHEST
        )
        on_diag = (jnp.arange(per_dev, dtype=jnp.int32) == step_local_row) & (row_index == step_row)
        new_column = row_panel + jnp.where(on_diag[:, None, None], chol[None], 0.0)
        old_column = lax.dynamic_slice(
            factor, (zero, zero, step_local_col, zero), (per_dev, width, 1, width)
        ).reshape(per_dev, width, width)
        kept = jnp.where(col_index == step_col, new_column, old_column)
        factor = lax.dynamic_update_slice(
            factor, kept.reshape(per_dev, width, 1, width), (zero, zero, step_local_col, zero)
        )
        pivots = lax.dynamic_update_slice(pivots, chol[None], (step, zero, zero))
        return (working, factor, pivots)

    start_state = (matrix, jnp.zeros_like(matrix), jnp.zeros((nblock, width, width), jnp.float32))
    _, factor, pivots = lax.fori_loop(0, nblock, factor_step, start_state)
    shaped = factor.reshape(1, per_dev, width, 1, per_dev, width)
    across = lax.all_gather(shaped, "gy", axis=3, tiled=True)
    whole = lax.all_gather(across, "gx", axis=0, tiled=True)
    lower = whole.transpose(1, 0, 2, 4, 3, 5).reshape(nblock * width, nblock * width)
    middle = jax.scipy.linalg.solve_triangular(lower, rhs.reshape(-1), lower=True)
    answer = jax.scipy.linalg.solve_triangular(lower, middle, lower=True, trans=1)
    solution = answer.reshape(nblock, width)
    return (factor.reshape(1, per_dev, width, 1, per_dev, width), solution)


def solution(mesh):
    in_specs = (
        P(("gx", "gy", "gz"), None),
        P(("gx", "gy", "gz"), None, None),
        P(("gx", "gy", "gz")),
    )
    out_specs = (P("gx", None, None, "gy", None, None), P())
    return jax.shard_map(
        on_device, mesh=mesh, in_specs=in_specs, out_specs=out_specs, check_vma=False
    )
```

profile of v0, /device:TPU:1, one launch (start us, length us, event | category | flops | bytes accessed | tf_op | source)
XLA Modules:
  0.0 2133.1 jit_solution(3347520525819320981)
XLA Ops:
  25.3 16.4 copy.39
  42.0 311.7 %reduce-scatter.2.cloned.1.call-done = f32[1,2,128,2,128]{4,2,3,1,0:T(8,128)} async-done(((f32[64,2,128,2,128]{4,2,3,1,0:T(8,128)}), f32[1,2,128,2,128]{4,2,3,1,0:T(8,128)}) %reduce-scatter.2.cloned.1.call-update) | async-done | bytes 262160 | tf_op jit(solution)/shard_map/reduce_scatter | solution.py:58
  353.8 35.4 %all-reduce.2.cloned.1.call-done = f32[2,128,2,128]{3,1,2,0:T(8,128)} async-done(((f32[2,128,2,128]{3,1,2,0:T(8,128)}), f32[2,128,2,128]{3,1,2,0:T(8,128)}) %all-reduce.2.cloned.1.call-update) | async-done | bytes 262160 | tf_op jit(solution)/shard_map/psum | solution.py:59
  389.2 1176.2 %while.20 = (s32[]{:T(128)}, f32[2,128,2,128]{3,1,2,0:T(8,128)}, f32[2,128,2,128]{3,1,0,2:T(8,128)S(1)}, s32[]{:T(128)}, s32[]{:T(128)}, /*index=5*/s32[]{:T(128...) while((s32[]{:T(128)}, f32[2,128,2,128]{3,1,2,0:T(8,128)}, ...), condition=%wide.region_5.6_spmd.clone, body=%wide.region_2.5_spmd.clone.sunk | while | flops 503890112 | bytes 12519428 | solution.py:104
  391.0 25.2 %all-gather.13.cloned.1.call-done = f32[16,128,1,128]{3,1,2,0:T(8,128)} async-done(((f32[2,128,1,128]{3,1,2,0:T(8,128)}), f32[16,128,1,128]{3,1,2,0:T(8,128)}) %all-gather.13.cloned.1.call-update) | async-done | bytes 1048592 | tf_op jit(solution)/shard_map/while/body/eval_jaxpr/all_gather | solution.py:11
  423.0 15.8 all-to-all-done
  466.8 22.6 %all-gather.13.cloned.1.call-done = f32[16,128,1,128]{3,1,2,0:T(8,128)} async-done(((f32[2,128,1,128]{3,1,2,0:T(8,128)}), f32[16,128,1,128]{3,1,2,0:T(8,128)}) %all-gather.13.cloned.1.call-update) | async-done | bytes 1048592 | tf_op jit(solution)/shard_map/while/body/eval_jaxpr/all_gather | solution.py:11
  496.3 15.8 all-to-all-done
  540.0 22.6 %all-gather.13.cloned.1.call-done = f32[16,128,1,128]{3,1,2,0:T(8,128)} async-done(((f32[2,128,1,128]{3,1,2,0:T(8,128)}), f32[16,128,1,128]{3,1,2,0:T(8,128)}) %all-gather.13.cloned.1.call-update) | async-done | bytes 1048592 | tf_op jit(solution)/shard_map/while/body/eval_jaxpr/all_gather | solution.py:11
  569.5 15.8 all-to-all-done
  613.3 22.6 %all-gather.13.cloned.1.call-done = f32[16,128,1,128]{3,1,2,0:T(8,128)} async-done(((f32[2,128,1,128]{3,1,2,0:T(8,128)}), f32[16,128,1,128]{3,1,2,0:T(8,128)}) %all-gather.13.cloned.1.call-update) | async-done | bytes 1048592 | tf_op jit(solution)/shard_map/while/body/eval_jaxpr/all_gather | solution.py:11
  642.8 15.8 all-to-all-done
  686.5 22.9 %all-gather.13.cloned.1.call-done = f32[16,128,1,128]{3,1,2,0:T(8,128)} async-done(((f32[2,128,1,128]{3,1,2,0:T(8,128)}), f32[16,128,1,128]{3,1,2,0:T(8,128)}) %all-gather.13.cloned.1.call-update) | async-done | bytes 1048592 | tf_op jit(solution)/shard_map/while/body/eval_jaxpr/all_gather | solution.py:11
  716.4 15.8 all-to-all-done
  760.1 22.9 %all-gather.13.cloned.1.call-done = f32[16,128,1,128]{3,1,2,0:T(8,128)} async-done(((f32[2,128,1,128]{3,1,2,0:T(8,128)}), f32[16,128,1,128]{3,1,2,0:T(8,128)}) %all-gather.13.cloned.1.call-update) | async-done | bytes 1048592 | tf_op jit(solution)/shard_map/while/body/eval_jaxpr/all_gather | solution.py:11
  833.6 22.9 %all-gather.13.cloned.1.call-done = f32[16,128,1,128]{3,1,2,0:T(8,128)} async-done(((f32[2,128,1,128]{3,1,2,0:T(8,128)}), f32[16,128,1,128]{3,1,2,0:T(8,128)}) %all-gather.13.cloned.1.call-update) | async-done | bytes 1048592 | tf_op jit(solution)/shard_map/while/body/eval_jaxpr/all_gather | solution.py:11
  907.2 22.6 %all-gather.13.cloned.1.call-done = f32[16,128,1,128]{3,1,2,0:T(8,128)} async-done(((f32[2,128,1,128]{3,1,2,0:T(8,128)}), f32[16,128,1,128]{3,1,2,0:T(8,128)}) %all-gather.13.cloned.1.call-update) | async-done | bytes 1048592 | tf_op jit(solution)/shard_map/while/body/eval_jaxpr/all_gather | solution.py:11
  936.7 15.8 all-to-all-done
  980.5 22.9 %all-gather.13.cloned.1.call-done = f32[16,128,1,128]{3,1,2,0:T(8,128)} async-done(((f32[2,128,1,128]{3,1,2,0:T(8,128)}), f32[16,128,1,128]{3,1,2,0:T(8,128)}) %all-gather.13.cloned.1.call-update) | async-done | bytes 1048592 | tf_op jit(solution)/shard_map/while/body/eval_jaxpr/all_gather | solution.py:11
  1054.0 22.6 %all-gather.13.cloned.1.call-done = f32[16,128,1,128]{3,1,2,0:T(8,128)} async-done(((f32[2,128,1,128]{3,1,2,0:T(8,128)}), f32[16,128,1,128]{3,1,2,0:T(8,128)}) %all-gather.13.cloned.1.call-update) | async-done | bytes 1048592 | tf_op jit(solution)/shard_map/while/body/eval_jaxpr/all_gather | solution.py:11
  1127.3 22.9 %all-gather.13.cloned.1.call-done = f32[16,128,1,128]{3,1,2,0:T(8,128)} async-done(((f32[2,128,1,128]{3,1,2,0:T(8,128)}), f32[16,128,1,128]{3,1,2,0:T(8,128)}) %all-gather.13.cloned.1.call-update) | async-done | bytes 1048592 | tf_op jit(solution)/shard_map/while/body/eval_jaxpr/all_gather | solution.py:11
  1200.8 22.6 %all-gather.13.cloned.1.call-done = f32[16,128,1,128]{3,1,2,0:T(8,128)} async-done(((f32[2,128,1,128]{3,1,2,0:T(8,128)}), f32[16,128,1,128]{3,1,2,0:T(8,128)}) %all-gather.13.cloned.1.call-update) | async-done | bytes 1048592 | tf_op jit(solution)/shard_map/while/body/eval_jaxpr/all_gather | solution.py:11
  1274.1 22.6 %all-gather.13.cloned.1.call-done = f32[16,128,1,128]{3,1,2,0:T(8,128)} async-done(((f32[2,128,1,128]{3,1,2,0:T(8,128)}), f32[16,128,1,128]{3,1,2,0:T(8,128)}) %all-gather.13.cloned.1.call-update) | async-done | bytes 1048592 | tf_op jit(solution)/shard_map/while/body/eval_jaxpr/all_gather | solution.py:11
  1303.6 15.8 all-to-all-done
  1347.4 22.6 %all-gather.13.cloned.1.call-done = f32[16,128,1,128]{3,1,2,0:T(8,128)} async-done(((f32[2,128,1,128]{3,1,2,0:T(8,128)}), f32[16,128,1,128]{3,1,2,0:T(8,128)}) %all-gather.13.cloned.1.call-update) | async-done | bytes 1048592 | tf_op jit(solution)/shard_map/while/body/eval_jaxpr/all_gather | solution.py:11
  1420.6 22.6 %all-gather.13.cloned.1.call-done = f32[16,128,1,128]{3,1,2,0:T(8,128)} async-done(((f32[2,128,1,128]{3,1,2,0:T(8,128)}), f32[16,128,1,128]{3,1,2,0:T(8,128)}) %all-gather.13.cloned.1.call-update) | async-done | bytes 1048592 | tf_op jit(solution)/shard_map/while/body/eval_jaxpr/all_gather | solution.py:11
  1493.9 22.6 %all-gather.13.cloned.1.call-done = f32[16,128,1,128]{3,1,2,0:T(8,128)} async-done(((f32[2,128,1,128]{3,1,2,0:T(8,128)}), f32[16,128,1,128]{3,1,2,0:T(8,128)}) %all-gather.13.cloned.1.call-update) | async-done | bytes 1048592 | tf_op jit(solution)/shard_map/while/body/eval_jaxpr/all_gather | solution.py:11
  1566.2 25.3 %all-gather.11.cloned.1.call-done = f32[2,128,16,128]{3,1,0,2:T(8,128)} async-done(((f32[2,128,2,128]{3,1,0,2:T(8,128)}), f32[2,128,16,128]{3,1,0,2:T(8,128)}) %all-gather.11.cloned.1.call-update) | async-done | bytes 2097168 | tf_op jit(solution)/shard_map/all_gather | solution.py:106
  1599.6 214.9 %psum.15 = f32[16,128]{1,0:T(8,128)S(1)} all-reduce(f32[16,128]{1,0:T(8,128)S(1)} %fusion.19), channel_id=1, replica_groups=mesh['gx'=8,'gy'=8,'gz'=2] {'gx','gy','gz'}, use_global_device_ids=true, to_apply=%region_6.7 | all-reduce | flops 2048 | bytes 16384 | tf_op jit(solution)/shard_map/psum | solution.py:52
  1827.8 18.0 reshape.532
  1858.2 56.3 %while.19 = (s32[]{:T(128)}, f32[2048,2048]{1,0:T(8,128)}, s32[16,2]{0,1:T(2,128)S(1)}, f32[16,128,128]{2,1,0:T(8,128)}, s32[]{:T(128)}) while((s32[]{:T(128)}, f32[2048,2048]{1,0:T(8,128)}, s32[16,2]{0,1:T(2,128)S(1)}, f32[16,128,128]{2,1,0:T(8,128)}, s32[]{:T(128)}) %tuple.184), condition=%wide.while_cond, body=%wide.while_body.sunk | while | flops 2 | bytes 132705 | solution.py:110
  1914.5 157.9 %custom-call.28 = f32[16,128,128]{1,2,0:T(8,128)S(1)} custom-call(f32[16,128,128]{2,1,0:T(8,128)} %get-tuple-element.183), custom_call_target="InvertDiagBlocksLowerTriangular" | custom-call | tf_op jit(solution)/shard_map/jit(_solve_triangular)/triangular_solve | solution.py:110
  (573 shorter events, 860.1 us)
Async XLA Ops:
  7.2 346.6 %reduce-scatter.2.cloned.1.call-start = ((), (), s32[]{:S(2)}) async-start(), calls=%async_computation.2 | async-start | bytes 17039360 | tf_op jit(solution)/shard_map/reduce_scatter | solution.py:58
  41.8 347.4 %all-reduce.2.cloned.1.call-start = ((), (), s32[]{:S(2)}) async-start(), calls=%async_computation.3 | async-start | bytes 524288 | tf_op jit(solution)/shard_map/psum | solution.py:59
  389.2 26.9 %all-gather.13.cloned.1.call-start = ((), (), s32[]{:S(2)}) async-start(), calls=%async_computation.6 | async-start | bytes 1179648 | tf_op jit(solution)/shard_map/while/body/eval_jaxpr/all_gather | solution.py:11
  418.1 20.8 all-to-all-start
  465.1 24.3 %all-gather.13.cloned.1.call-start = ((), (), s32[]{:S(2)}) async-start(), calls=%async_computation.6 | async-start | bytes 1179648 | tf_op jit(solution)/shard_map/while/body/eval_jaxpr/all_gather | solution.py:11
  538.3 24.3 %all-gather.13.cloned.1.call-start = ((), (), s32[]{:S(2)}) async-start(), calls=%async_computation.6 | async-start | bytes 1179648 | tf_op jit(solution)/shard_map/while/body/eval_jaxpr/all_gather | solution.py:11
  564.6 20.8 all-to-all-start
  611.6 24.3 %all-gather.13.cloned.1.call-start = ((), (), s32[]{:S(2)}) async-start(), calls=%async_computation.6 | async-start | bytes 1179648 | tf_op jit(solution)/shard_map/while/body/eval_jaxpr/all_gather | solution.py:11
  637.9 20.8 all-to-all-start
  684.8 24.6 %all-gather.13.cloned.1.call-start = ((), (), s32[]{:S(2)}) async-start(), calls=%async_computation.6 | async-start | bytes 1179648 | tf_op jit(solution)/shard_map/while/body/eval_jaxpr/all_gather | solution.py:11
  758.4 24.6 %all-gather.13.cloned.1.call-start = ((), (), s32[]{:S(2)}) async-start(), calls=%async_computation.6 | async-start | bytes 1179648 | tf_op jit(solution)/shard_map/while/body/eval_jaxpr/all_gather | solution.py:11
  785.0 20.8 all-to-all-start
  832.0 24.6 %all-gather.13.cloned.1.call-start = ((), (), s32[]{:S(2)}) async-start(), calls=%async_computation.6 | async-start | bytes 1179648 | tf_op jit(solution)/shard_map/while/body/eval_jaxpr/all_gather | solution.py:11
  858.6 20.8 all-to-all-start
  905.5 24.3 %all-gather.13.cloned.1.call-start = ((), (), s32[]{:S(2)}) async-start(), calls=%async_computation.6 | async-start | bytes 1179648 | tf_op jit(solution)/shard_map/while/body/eval_jaxpr/all_gather | solution.py:11
  978.8 24.6 %all-gather.13.cloned.1.call-start = ((), (), s32[]{:S(2)}) async-start(), calls=%async_computation.6 | async-start | bytes 1179648 | tf_op jit(solution)/shard_map/while/body/eval_jaxpr/all_gather | solution.py:11
  1005.4 20.8 all-to-all-start
  1052.4 24.3 %all-gather.13.cloned.1.call-start = ((), (), s32[]{:S(2)}) async-start(), calls=%async_computation.6 | async-start | bytes 1179648 | tf_op jit(solution)/shard_map/while/body/eval_jaxpr/all_gather | solution.py:11
  1078.6 20.8 all-to-all-start
  1125.6 24.6 %all-gather.13.cloned.1.call-start = ((), (), s32[]{:S(2)}) async-start(), calls=%async_computation.6 | async-start | bytes 1179648 | tf_op jit(solution)/shard_map/while/body/eval_jaxpr/all_gather | solution.py:11
  1152.2 20.8 all-to-all-start
  1199.2 24.3 %all-gather.13.cloned.1.call-start = ((), (), s32[]{:S(2)}) async-start(), calls=%async_computation.6 | async-start | bytes 1179648 | tf_op jit(solution)/shard_map/while/body/eval_jaxpr/all_gather | solution.py:11
  1225.4 20.8 all-to-all-start
  1272.4 24.3 %all-gather.13.cloned.1.call-start = ((), (), s32[]{:S(2)}) async-start(), calls=%async_computation.6 | async-start | bytes 1179648 | tf_op jit(solution)/shard_map/while/body/eval_jaxpr/all_gather | solution.py:11
  1298.7 20.8 all-to-all-start
  1345.7 24.3 %all-gather.13.cloned.1.call-start = ((), (), s32[]{:S(2)}) async-start(), calls=%async_computation.6 | async-start | bytes 1179648 | tf_op jit(solution)/shard_map/while/body/eval_jaxpr/all_gather | solution.py:11
  1372.0 20.8 all-to-all-start
  1418.9 24.3 %all-gather.13.cloned.1.call-start = ((), (), s32[]{:S(2)}) async-start(), calls=%async_computation.6 | async-start | bytes 1179648 | tf_op jit(solution)/shard_map/while/body/eval_jaxpr/all_gather | solution.py:11
  1445.2 20.8 all-to-all-start
  1492.2 24.3 %all-gather.13.cloned.1.call-start = ((), (), s32[]{:S(2)}) async-start(), calls=%async_computation.6 | async-start | bytes 1179648 | tf_op jit(solution)/shard_map/while/body/eval_jaxpr/all_gather | solution.py:11
  1565.4 26.1 %all-gather.11.cloned.1.call-start = ((), (), s32[]{:S(2)}) async-start(), calls=%async_computation.5 | async-start | bytes 2359296 | tf_op jit(solution)/shard_map/all_gather | solution.py:106
  1566.2 250.1 %all-gather.9.cloned.1.call-start = ((), (), s32[]{:S(2)}) async-start(), calls=%async_computation.4 | async-start | bytes 18874368 | tf_op jit(solution)/shard_map/all_gather | solution.py:107
  (9 other events, 3707.0 us)
Sparse Core Ops, SparseCore 0:
  41.9 311.8 reduce-scatter.1
  356.2 32.9 all-reduce.1
  392.3 23.7 all-gather.12
  467.9 21.4 all-gather.12
  541.1 21.4 all-gather.12
  614.4 21.4 all-gather.12
  688.0 21.4 all-gather.12
  761.5 21.4 all-gather.12
  835.1 21.4 all-gather.12
  908.3 21.4 all-gather.12
  981.9 21.4 all-gather.12
  1055.1 21.4 all-gather.12
  1128.7 21.4 all-gather.12
  1202.0 21.4 all-gather.12
  1275.2 21.4 all-gather.12
  1348.5 21.4 all-gather.12
  1421.7 21.4 all-gather.12
  1495.0 21.4 all-gather.12
  1568.0 23.5 all-gather.10
  1595.8 170.8 all-gather.8
where the time goes:
time: 2140 us; the launch traced here: 2130 us
  waiting for transfers between devices  992 us (46%)
  other arithmetic  543 us (25%)
  blocking collectives  215 us (10%)
  local copies, waits for them, and re-layouts  170 us (8%)
  matrix products  116 us (5%)
  starting transfers between devices  79.4 us (4%)
    all_gather x16, waiting for transfers between devices, picked(): lax.all_gather(x, axis)  366 us
    reduce_scatter x1, waiting for transfers between devices, on_device(): lax.psum_scatter(blockwise, ('gx', 'gy'), scatter_dimension=0, tiled=True)  312 us
    all_to_all x16, waiting for transfers between devices, copy_for_each(): lax.all_to_all(jnp.broadcast_to(x[None], (size, *x.shape)), axis, 0, 0, t...  253 us
    psum x1, blocking collectives, on_device(): rhs = lax.psum(rhs_local, ('gx', 'gy', 'gz'))  215 us
    another operation x48, other arithmetic, factor_step(): chol = jnp.linalg.cholesky(own_diag)  199 us
    another operation x3, other arithmetic, on_device(): jax.scipy.linalg.solve_triangular(lower, middle, lower=True, trans=1)  170 us
    another operation x32, other arithmetic, factor_step(): solved = jax.scipy.linalg.solve_triangular(chol, stacked, lower=True)  168 us
    all_to_all x16, starting transfers between devices, copy_for_each(): lax.all_to_all(jnp.broadcast_to(x[None], (size, *x.shape)), axis, 0, 0, t...  78.3 us
  transfers between devices with their start and end apart: 36, of which 35 were waited for; matrix products, arithmetic and copies ran while one was open for 0% of the time, Pallas kernels for 0%

commit v1 on v0

--- a/solution.py
+++ b/solution.py
@@ -49,7 +49,7 @@
     rhs_local = (
         jnp.einsum("osb,osx->bx", natural, weighted, precision=lax.Precision.HIGHEST) * scale
     )
-    rhs = lax.psum(rhs_local, ("gx", "gy", "gz"))
+    rhs = jnp.sum(lax.all_gather(rhs_local, ("gx", "gy", "gz")), axis=0)
     row_span = min(row_count, (1 * lax.axis_size(("gx", "gy")) - 1) // col_count + 2)
     blockwise = (
         jnp.einsum("opix,oqjy->pqixjy", design, design, preferred_element_type=jnp.float32) * scale

time: 2140 us -> 2380 us (1.11)
  waiting for transfers between devices: 992 us -> 1460 us
  blocking collectives: 215 us -> 0 us
    all_gather x0 -> x1, waiting for transfers between devices: none -> 299 us  [on_device(): rhs = jnp.sum(lax.all_gather(rhs_local, ('gx', 'gy', 'gz')), axis=0)]
    psum x1 -> x0, blocking collectives: 215 us -> none  [on_device(): rhs = lax.psum(rhs_local, ('gx', 'gy', 'gz'))]
    all_gather x1, waiting for transfers between devices: 0.01 us -> 169 us  [on_device(): whole = lax.all_gather(across, 'gx', axis=0, tiled=True)]
  transfers between devices with their start and end apart: 36 -> 37, of which waited for: 35 -> 37; matrix products, arithmetic and copies ran while one was open for 0% -> 1% of each run, Pallas kernels for 0% -> 0%
where the time goes in v1:
time: 2380 us; the launch traced here: 2370 us
  waiting for transfers between devices  1460 us (61%)
  other arithmetic  542 us (23%)
  local copies, waits for them, and re-layouts  160 us (7%)
  matrix products  117 us (5%)
  starting transfers between devices  79.6 us (3%)
    all_gather x16, waiting for transfers between devices, picked(): lax.all_gather(x, axis)  366 us
    reduce_scatter x1, waiting for transfers between devices, on_device(): lax.psum_scatter(blockwise, ('gx', 'gy'), scatter_dimension=0, tiled=True)  312 us
    all_gather x1, waiting for transfers between devices, on_device(): rhs = jnp.sum(lax.all_gather(rhs_local, ('gx', 'gy', 'gz')), axis=0)  299 us
    all_to_all x16, waiting for transfers between devices, copy_for_each(): lax.all_to_all(jnp.broadcast_to(x[None], (size, *x.shape)), axis, 0, 0, t...  253 us
    another operation x48, other arithmetic, factor_step(): chol = jnp.linalg.cholesky(own_diag)  198 us
    another operation x3, other arithmetic, on_device(): jax.scipy.linalg.solve_triangular(lower, middle, lower=True, trans=1)  170 us
    all_gather x1, waiting for transfers between devices, on_device(): whole = lax.all_gather(across, 'gx', axis=0, tiled=True)  169 us
    another operation x32, other arithmetic, factor_step(): solved = jax.scipy.linalg.solve_triangular(chol, stacked, lower=True)  167 us
  transfers between devices with their start and end apart: 37, of which 37 were waited for; matrix products, arithmetic and copies ran while one was open for 1% of the time, Pallas kernels for 0%

profile of v1, /device:TPU:1, one launch (start us, length us, event | category | flops | bytes accessed | tf_op | source)
XLA Modules:
  0.0 2371.8 jit_solution(4316519583966928411)
XLA Ops:
  25.3 16.4 copy.39
  42.0 311.7 %reduce-scatter.2.cloned.1.call-done = f32[1,2,128,2,128]{4,2,3,1,0:T(8,128)} async-done(((f32[64,2,128,2,128]{4,2,3,1,0:T(8,128)}), f32[1,2,128,2,128]{4,2,3,1,0:T(8,128)}) %reduce-scatter.2.cloned.1.call-update) | async-done | bytes 262160 | tf_op jit(solution)/shard_map/reduce_scatter | solution.py:58
  353.8 35.4 %all-reduce.2.cloned.1.call-done = f32[2,128,2,128]{3,1,2,0:T(8,128)} async-done(((f32[2,128,2,128]{3,1,2,0:T(8,128)}), f32[2,128,2,128]{3,1,2,0:T(8,128)}) %all-reduce.2.cloned.1.call-update) | async-done | bytes 262160 | tf_op jit(solution)/shard_map/psum | solution.py:59
  389.2 1174.6 %while.20 = (s32[]{:T(128)}, f32[2,128,2,128]{3,1,2,0:T(8,128)}, f32[2,128,2,128]{3,1,0,2:T(8,128)S(1)}, s32[]{:T(128)}, s32[]{:T(128)}, /*index=5*/s32[]{:T(128...) while((s32[]{:T(128)}, f32[2,128,2,128]{3,1,2,0:T(8,128)}, ...), condition=%wide.region_5.6_spmd.clone, body=%wide.region_2.5_spmd.clone.sunk | while | flops 503890112 | bytes 12519428 | solution.py:104
  390.9 25.2 %all-gather.17.cloned.1.call-done = f32[16,128,1,128]{3,1,2,0:T(8,128)} async-done(((f32[2,128,1,128]{3,1,2,0:T(8,128)}), f32[16,128,1,128]{3,1,2,0:T(8,128)}) %all-gather.17.cloned.1.call-update) | async-done | bytes 1048592 | tf_op jit(solution)/shard_map/while/body/eval_jaxpr/all_gather | solution.py:11
  423.0 15.8 all-to-all-done
  466.6 22.6 all-gather.17.cloned.1.call-done
  539.8 22.6 all-gather.17.cloned.1.call-done
  612.9 22.6 all-gather.17.cloned.1.call-done
  642.5 15.8 all-to-all-done
  686.1 22.9 all-gather.17.cloned.1.call-done
  715.9 15.8 all-to-all-done
  759.6 22.9 all-gather.17.cloned.1.call-done
  833.0 22.9 all-gather.17.cloned.1.call-done
  906.5 22.6 all-gather.17.cloned.1.call-done
  979.7 22.9 all-gather.17.cloned.1.call-done
  1009.5 15.8 all-to-all-done
  1053.1 22.6 all-gather.17.cloned.1.call-done
  1082.6 15.8 all-to-all-done
  1126.3 22.9 all-gather.17.cloned.1.call-done
  1156.1 15.8 all-to-all-done
  1199.7 22.6 all-gather.17.cloned.1.call-done
  1272.9 22.6 all-gather.17.cloned.1.call-done
  1346.0 22.6 all-gather.17.cloned.1.call-done
  1419.2 22.6 all-gather.17.cloned.1.call-done
  1492.3 22.6 all-gather.17.cloned.1.call-done
  1569.4 20.6 all-gather.13.cloned.1.call-done
  1594.1 299.4 %all-gather.15.cloned.1.call-done = f32[2048,128]{1,0:T(8,128)} async-done(((f32[16,128]{1,0:T(8,128)}), f32[2048,128]{1,0:T(8,128)}) %all-gather.15.cloned.1.call-update) | async-done | bytes 1048592 | tf_op jit(solution)/shard_map/all_gather | solution.py:52
  1896.7 169.0 %all-gather.11.cloned.1.call-done = f32[8,2,128,8,2,128]{5,3,4,2,1,0:T(8,128)} async-done(((f32[1,2,128,8,2,128]{5,3,4,2,1,0:T(8,128)}), f32[8,2,128,8,2,128]{5,3,4,2,1,0:T(8,128)}) %all-gather.11.cloned.1.call-update) | async-done | bytes 16777232 | tf_op jit(solution)/shard_map/all_gather | solution.py:107
  2077.1 18.0 reshape.532
  2107.6 46.5 %while.19 = (s32[]{:T(128)}, f32[2048,2048]{1,0:T(8,128)}, s32[16,2]{0,1:T(2,128)S(1)}, f32[16,128,128]{2,1,0:T(8,128)S(1)}, s32[]{:T(128)}) while((s32[]{:T(128)}, f32[2048,2048]{1,0:T(8,128)}, s32[16,2]{0,1:T(2,128)S(1)}, f32[16,128,128]{2,1,0:T(8,128)S(1)}, s32[]{:T(128)}) %tuple.184), condition=%wide.while_cond, body=%wide.while_body.sunk | while | flops 2 | bytes 131181 | solution.py:110
  2154.1 157.2 %custom-call.28 = f32[16,128,128]{1,2,0:T(8,128)S(1)} custom-call(f32[16,128,128]{2,1,0:T(8,128)S(1)} %get-tuple-element.183), custom_call_target="InvertDiagBlocksLowerTriangular" | custom-call | tf_op jit(solution)/shard_map/jit(_solve_triangular)/triangular_solve | solution.py:110
  (576 shorter events, 866.5 us)
Async XLA Ops:
  7.2 346.6 %reduce-scatter.2.cloned.1.call-start = ((), (), s32[]{:S(2)}) async-start(), calls=%async_computation.2 | async-start | bytes 17039360 | tf_op jit(solution)/shard_map/reduce_scatter | solution.py:58
  41.8 347.4 %all-reduce.2.cloned.1.call-start = ((), (), s32[]{:S(2)}) async-start(), calls=%async_computation.3 | async-start | bytes 524288 | tf_op jit(solution)/shard_map/psum | solution.py:59
  389.2 26.9 %all-gather.17.cloned.1.call-start = ((), (), s32[]{:S(2)}) async-start(), calls=%async_computation.7 | async-start | bytes 1179648 | tf_op jit(solution)/shard_map/while/body/eval_jaxpr/all_gather | solution.py:11
  418.1 20.8 all-to-all-start
  465.0 24.3 %all-gather.17.cloned.1.call-start = ((), (), s32[]{:S(2)}) async-start(), calls=%async_computation.7 | async-start | bytes 1179648 | tf_op jit(solution)/shard_map/while/body/eval_jaxpr/all_gather | solution.py:11
  538.1 24.3 %all-gather.17.cloned.1.call-start = ((), (), s32[]{:S(2)}) async-start(), calls=%async_computation.7 | async-start | bytes 1179648 | tf_op jit(solution)/shard_map/while/body/eval_jaxpr/all_gather | solution.py:11
  611.3 24.3 %all-gather.17.cloned.1.call-start = ((), (), s32[]{:S(2)}) async-start(), calls=%async_computation.7 | async-start | bytes 1179648 | tf_op jit(solution)/shard_map/while/body/eval_jaxpr/all_gather | solution.py:11
  637.6 20.8 all-to-all-start
  684.4 24.6 %all-gather.17.cloned.1.call-start = ((), (), s32[]{:S(2)}) async-start(), calls=%async_computation.7 | async-start | bytes 1179648 | tf_op jit(solution)/shard_map/while/body/eval_jaxpr/all_gather | solution.py:11
  711.0 20.8 all-to-all-start
  757.9 24.6 %all-gather.17.cloned.1.call-start = ((), (), s32[]{:S(2)}) async-start(), calls=%async_computation.7 | async-start | bytes 1179648 | tf_op jit(solution)/shard_map/while/body/eval_jaxpr/all_gather | solution.py:11
  784.5 20.8 all-to-all-start
  831.4 24.6 %all-gather.17.cloned.1.call-start = ((), (), s32[]{:S(2)}) async-start(), calls=%async_computation.7 | async-start | bytes 1179648 | tf_op jit(solution)/shard_map/while/body/eval_jaxpr/all_gather | solution.py:11
  904.8 24.3 %all-gather.17.cloned.1.call-start = ((), (), s32[]{:S(2)}) async-start(), calls=%async_computation.7 | async-start | bytes 1179648 | tf_op jit(solution)/shard_map/while/body/eval_jaxpr/all_gather | solution.py:11
  978.0 24.6 %all-gather.17.cloned.1.call-start = ((), (), s32[]{:S(2)}) async-start(), calls=%async_computation.7 | async-start | bytes 1179648 | tf_op jit(solution)/shard_map/while/body/eval_jaxpr/all_gather | solution.py:11
  1004.6 20.8 all-to-all-start
  1051.4 24.3 %all-gather.17.cloned.1.call-start = ((), (), s32[]{:S(2)}) async-start(), calls=%async_computation.7 | async-start | bytes 1179648 | tf_op jit(solution)/shard_map/while/body/eval_jaxpr/all_gather | solution.py:11
  1077.7 20.8 all-to-all-start
  1124.6 24.6 %all-gather.17.cloned.1.call-start = ((), (), s32[]{:S(2)}) async-start(), calls=%async_computation.7 | async-start | bytes 1179648 | tf_op jit(solution)/shard_map/while/body/eval_jaxpr/all_gather | solution.py:11
  1151.2 20.8 all-to-all-start
  1198.1 24.3 %all-gather.17.cloned.1.call-start = ((), (), s32[]{:S(2)}) async-start(), calls=%async_computation.7 | async-start | bytes 1179648 | tf_op jit(solution)/shard_map/while/body/eval_jaxpr/all_gather | solution.py:11
  1224.3 20.8 all-to-all-start
  1271.2 24.3 %all-gather.17.cloned.1.call-start = ((), (), s32[]{:S(2)}) async-start(), calls=%async_computation.7 | async-start | bytes 1179648 | tf_op jit(solution)/shard_map/while/body/eval_jaxpr/all_gather | solution.py:11
  1297.5 20.8 all-to-all-start
  1344.4 24.3 %all-gather.17.cloned.1.call-start = ((), (), s32[]{:S(2)}) async-start(), calls=%async_computation.7 | async-start | bytes 1179648 | tf_op jit(solution)/shard_map/while/body/eval_jaxpr/all_gather | solution.py:11
  1370.6 20.8 all-to-all-start
  1417.5 24.3 %all-gather.17.cloned.1.call-start = ((), (), s32[]{:S(2)}) async-start(), calls=%async_computation.7 | async-start | bytes 1179648 | tf_op jit(solution)/shard_map/while/body/eval_jaxpr/all_gather | solution.py:11
  1490.7 24.3 %all-gather.17.cloned.1.call-start = ((), (), s32[]{:S(2)}) async-start(), calls=%async_computation.7 | async-start | bytes 1179648 | tf_op jit(solution)/shard_map/while/body/eval_jaxpr/all_gather | solution.py:11
  1517.0 20.8 all-to-all-start
  1563.8 26.1 %all-gather.13.cloned.1.call-start = ((), (), s32[]{:S(2)}) async-start(), calls=%async_computation.5 | async-start | bytes 2359296 | tf_op jit(solution)/shard_map/all_gather | solution.py:106
  1564.6 328.9 %all-gather.15.cloned.1.call-start = ((), (), s32[]{:S(2)}) async-start(), calls=%async_computation.6 | async-start | bytes 1056768 | tf_op jit(solution)/shard_map/all_gather | solution.py:52
  1569.1 496.6 %all-gather.11.cloned.1.call-start = ((), (), s32[]{:S(2)}) async-start(), calls=%async_computation.4 | async-start | bytes 18874368 | tf_op jit(solution)/shard_map/all_gather | solution.py:107
  (10 other events, 3634.5 us)
Sparse Core Ops, SparseCore 0:
  41.9 311.8 reduce-scatter.1
  356.2 32.9 all-reduce.1
  392.3 23.7 all-gather.16
  467.8 21.4 all-gather.16
  540.9 21.4 all-gather.16
  614.1 21.4 all-gather.16
  687.5 21.4 all-gather.16
  761.0 21.4 all-gather.16
  834.5 21.4 all-gather.16
  907.6 21.4 all-gather.16
  981.1 21.4 all-gather.16
  1054.2 21.4 all-gather.16
  1127.7 21.4 all-gather.16
  1200.8 21.4 all-gather.16
  1274.0 21.4 all-gather.16
  1347.2 21.4 all-gather.16
  1420.3 21.4 all-gather.16
  1493.5 21.4 all-gather.16
  1566.4 23.5 all-gather.12
  1592.0 301.4 all-gather.14
  1895.2 170.4 all-gather.10
